TPU v7x, 256 devices: a whole 4x4x8 slice. The times are simulated.
256 devices in a mesh: cluster: 64 (over x, z, core), dir: 4 (over y).
Axes of the slice: x: 4, y: 4, z: 8, core: 2. Of those that a mesh axis runs over, the one named last changes fastest.
Arguments:
- ray_code: int32 [1024, 524288], P('dir', 'cluster'), may hold values from 0 to 16, as said below
- occluder_list: int32 [64, 16], replicated, may hold values from 0 to 511, as said below
- list_count: int32 [64], replicated, may hold values from 1 to 16, 768 in all
- normal_azimuth: float32 [524288], P('cluster'), may hold values from -3.140625 to 3.140625
- normal_height: float32 [524288], P('cluster'), may hold values from -1 to 1
- albedo: float32 [524288], P('cluster'), may hold values from 0.2 to 1
- occluder_exit_radiance: bfloat16 [512, 81, 1024], P('cluster', None, 'dir'), may hold values from -18 to 18
Outputs:
- transfer: bfloat16 [81, 524288], P(None, ('cluster', 'dir'))
Inputs may be any that keep to these rules, and one draw needn't show every extreme that they name: `occluder_list`: each row names 16 different blocks, exactly 2 held by each of 8 different clusters; block b is held by cluster b // 8. `list_count`: entry c is the number of leading slots of row c of occluder_list in use. `ray_code`: A code of a vertex of cluster c below list_count[c] names the slot of that cluster's list whose block the ray ends on; any other code means the ray escapes.
All inputs are finite; a program needn't handle non-finite values.
Results may differ from a plain program's by a relative error of at most 0.0041.
Values may be sent and summed in bfloat16 or wider, within the bound.
A program may use at most 128 MiB of HBM per device.

v0:
```python
import math
import jax
import jax.numpy as jnp
from jax import lax
from jax.sharding import PartitionSpec as P

NDIR = 1024
SHORD = 9
golden_angle = math.pi * (3.0 - math.sqrt(5.0))


def sphere_points(direction_index, direction_overall_count):
    position = direction_index.astype(jnp.float32)
    along_z = 1.0 - (2.0 * position + 1.0) / direction_overall_count
    radius = jnp.sqrt(jnp.maximum(1.0 - along_z * along_z, 0.0))
    turned = position * golden_angle
    return (radius * jnp.cos(turned), radius * jnp.sin(turned), along_z)


def harmonic_table(along_x, along_y, along_z, degrees):
    cosine_terms = [jnp.ones_like(along_x)]
    sine_terms = [jnp.zeros_like(along_x)]
    for power_exponent in range(1, degrees):
        cosine_terms.append(cosine_terms[-1] * along_x - sine_terms[-1] * along_y)
        sine_terms.append(cosine_terms[-2] * along_y + sine_terms[-1] * along_x)
    basis_rows = [None] * (degrees * degrees)
    for order_index in range(degrees):
        diagonal_entries = 1.0
        for factor in range(1, 2 * order_index, 2):
            diagonal_entries = diagonal_entries * factor
        legendre = [None] * degrees
        legendre[order_index] = jnp.full_like(along_z, diagonal_entries)
        if order_index + 1 < degrees:
            legendre[order_index + 1] = along_z * ((2 * order_index + 1) * diagonal_entries)
        for degree in range(order_index + 2, degrees):
            legendre[degree] = (
                (2 * degree - 1) * along_z * legendre[degree - 1]
                - (degree + order_index - 1) * legendre[degree - 2]
            ) / (degree - order_index)
        for degree in range(order_index, degrees):
            factor_norm = math.sqrt(
                (2 * degree + 1)
                / (4.0 * math.pi)
                * math.factorial(degree - order_index)
                / math.factorial(degree + order_index)
            )
            centre = degree * degree + degree
            if order_index == 0:
                basis_rows[centre] = factor_norm * legendre[degree]
            else:
                basis_rows[centre + order_index] = (
                    math.sqrt(2.0) * factor_norm * legendre[degree] * cosine_terms[order_index]
                )
                basis_rows[centre - order_index] = (
                    math.sqrt(2.0) * factor_norm * legendre[degree] * sine_terms[order_index]
                )
    return jnp.stack(basis_rows)


def facing_table(normal_azimuth, normal_height, along_x, along_y, along_z):
    planar = jnp.sqrt(jnp.maximum(1.0 - normal_height * normal_height, 0.0))
    normal_x = planar * jnp.cos(normal_azimuth)
    normal_y = planar * jnp.sin(normal_azimuth)
    return jnp.maximum(
        along_x[:, None] * normal_x[None, :]
        + along_y[:, None] * normal_y[None, :]
        + along_z[:, None] * normal_height[None, :],
        0.0,
    )


def per_device(
    ray_code,
    occluder_list,
    list_count,
    normal_azimuth,
    normal_height,
    albedo,
    occluder_exit_radiance,
):
    dir_total, vertex_total = ray_code.shape
    blocks_held, coeff_total = (occluder_exit_radiance.shape[0], occluder_exit_radiance.shape[1])
    clusters, slot_total = occluder_list.shape
    own_cluster = lax.axis_index("cluster")
    first_dir = lax.axis_index("dir") * dir_total
    along_x, along_y, along_z = sphere_points(first_dir + lax.iota(jnp.int32, dir_total), NDIR)
    harmonics = harmonic_table(along_x, along_y, along_z, SHORD)
    facing = facing_table(normal_azimuth, normal_height, along_x, along_y, along_z)
    live_count = list_count[own_cluster]
    occluded = ray_code < live_count
    direct = jnp.dot(
        harmonics,
        jnp.where(occluded, 0.0, facing),
        precision=lax.Precision.HIGHEST,
        preferred_element_type=jnp.float32,
    )
    own_list = occluder_list[own_cluster]
    slot_index = lax.iota(jnp.int32, slot_total)
    portion_slice = lax.all_gather(occluder_exit_radiance, "cluster", axis=0, tiled=True)
    selected_entries = own_list[:, None] == lax.iota(jnp.int32, portion_slice.shape[0])[None, :]
    entries = jnp.einsum(
        "fx,xwn->fwn",
        selected_entries.astype(jnp.bfloat16),
        portion_slice,
        preferred_element_type=jnp.float32,
    ).astype(jnp.bfloat16)
    stacked = jnp.transpose(entries, (1, 0, 2)).reshape(coeff_total, slot_total * dir_total)
    block_width = min(512, vertex_total)
    block_count = vertex_total // block_width

    def one_block(block_index):
        first_vertex = block_index * block_width
        ray_codes = lax.dynamic_slice_in_dim(ray_code, first_vertex, block_width, 1)
        lit = lax.dynamic_slice_in_dim(facing, first_vertex, block_width, 1)
        weight = jnp.where(ray_codes < live_count, lit, 0.0)
        onehot = ray_codes[None, :, :] == slot_index[:, None, None]
        spread = (
            jnp.where(onehot, weight[None, :, :], 0.0)
            .astype(jnp.bfloat16)
            .reshape(slot_total * dir_total, block_width)
        )
        return jnp.dot(stacked, spread, preferred_element_type=jnp.float32)

    pieces = lax.map(one_block, lax.iota(jnp.int32, block_count))
    bounce = jnp.transpose(pieces, (1, 0, 2)).reshape(coeff_total, vertex_total)
    partial_sum = 4.0 * math.pi / NDIR * (direct + albedo[None, :] * bounce)
    summed = lax.psum_scatter(partial_sum, "dir", scatter_dimension=1, tiled=True)
    return summed.astype(jnp.bfloat16)


def solution(mesh):
    return jax.shard_map(
        per_device,
        mesh=mesh,
        in_specs=(
            P("dir", "cluster"),
            P(),
            P(),
            P("cluster"),
            P("cluster"),
            P("cluster"),
            P("cluster", None, "dir"),
        ),
        out_specs=P(None, ("cluster", "dir")),
        check_vma=False,
    )
```

profile of v0, /device:TPU:1, one launch (start us, length us, event | category | flops | bytes accessed | tf_op | source)
XLA Modules:
  0.0 316.4 jit_solution(9582630595501091377)
XLA Ops:
  12.7 4.3 %add_maximum_fusion = bf16[256,8192]{1,0:T(8,128)(2,1)} fusion(f32[8192]{0:T(1024)} %param.13, f32[256]{0:T(256)S(1)} %multiply_subtract_fusion, f32[8192]{0:T(1024)S(1)} %get-tuple-element.99, f32[256]{0:T(256)S(1)} %get-tuple-element.100, f32[8192]{0:T(1024)S(1)} %get-tuple-element.98, f32[256]{0:T(256)S(1)} %get-tuple-element.101), kind=kLoop, calls=%fused_computation.11 | loop fusion | flops 14680064 | bytes 4295680 | tf_op jit(solution)/shard_map/max | solution.py:64
  17.0 115.2 %all-gather.2.cloned.1.call-done = bf16[512,81,256]{2,0,1:T(8,128)(2,1)} async-done(((bf16[8,81,256]{2,0,1:T(8,128)(2,1)}), bf16[512,81,256]{2,0,1:T(8,128)(2,1)}) %all-gather.2.cloned.1.call-update) | async-done | bytes 21233680 | tf_op jit(solution)/shard_map/all_gather | solution.py:99
  132.1 10.0 %fusion.7 = bf16[81,16,256]{2,1,0:T(8,128)(2,1)S(1)} fusion(bf16[512,81,256]{2,0,1:T(8,128)(2,1)} %all-gather.2.cloned.1.call-done, s32[16]{0:T(128)S(1)} %dynamic-slice_reduce_fusion), kind=kOutput, calls=%fused_computation.16 | convolution fusion | flops 340078592 | bytes 21897280 | tf_op jit(solution)/shard_map/fx,xwn->fwn/dot_general | solution.py:101
  142.5 114.1 %while.12 = (s32[]{:T(128)}, f32[16,81,512]{2,1,0:T(8,128)}, s32[16]{0:T(128)S(1)}, s32[256,8192]{1,0:T(8,128)}, s32[]{:T(128)}, /*index=5*/bf16[256,8192]{1,0:T...) while((s32[]{:T(128)}, f32[16,81,512]{2,1,0:T(8,128)}, ...), condition=%wide.region_1.2_spmd.clone, body=%wide.region_0.1_spmd.clone.sunk | while | flops 344195072 | bytes 12181759 | solution.py:124
  143.8 1.8 dynamic-slice_select_fusion.2
  151.0 1.8 dynamic-slice_select_fusion.2
  158.1 1.8 dynamic-slice_select_fusion.2
  165.2 1.8 dynamic-slice_select_fusion.2
  172.4 1.8 dynamic-slice_select_fusion.2
  179.5 1.8 dynamic-slice_select_fusion.2
  186.6 1.8 dynamic-slice_select_fusion.2
  193.8 1.8 dynamic-slice_select_fusion.2
  200.9 1.8 dynamic-slice_select_fusion.2
  208.0 1.8 dynamic-slice_select_fusion.2
  215.2 1.8 dynamic-slice_select_fusion.2
  222.3 1.8 dynamic-slice_select_fusion.2
  229.4 1.8 dynamic-slice_select_fusion.2
  236.6 1.8 dynamic-slice_select_fusion.2
  243.7 1.8 dynamic-slice_select_fusion.2
  256.6 3.5 %copy.9 = f32[81,16,512]{2,1,0:T(8,128)S(1)} copy(f32[81,16,512]{2,0,1:T(8,128)} %bitcast.55) | data formatting | bytes 5308416 | tf_op jit(solution)/shard_map/transpose | solution.py:125
  260.6 2.0 copy.12
  262.7 9.5 %fusion.2 = f32[81,8192]{1,0:T(8,128)} fusion(f32[81,256]{1,0:T(8,128)S(1)} %stack.5, s32[256,8192]{1,0:T(8,128)S(1)} %bitcast.54, s32[]{:T(128)} %bitcast, f32[81,8192]{1,0:T(8,128)S(1)} %bitcast.56, f32[8192]{0:T(1024)S(1)} %copy-done.2, f32[8192]{0:T(1024)S(1)} %copy-done.1, f32[256]{0:T(256)S(1)} %multiply_subtract_fusion, ...), kind=kOutput, calls=%fused_computation.9 | convolution fusion | flops 2057199616 | bytes 13914116 | tf_op jit(solution)/shard_map/dot_general | solution.py:91
  272.2 35.5 %reduce-scatter.2.cloned.1.call-done = f32[81,2048]{1,0:T(8,128)} async-done(((f32[81,8192]{1,0:T(8,128)}), f32[81,2048]{1,0:T(8,128)}) %reduce-scatter.2.cloned.1.call-update) | async-done | bytes 663568 | tf_op jit(solution)/shard_map/reduce_scatter | solution.py:127
  307.7 1.9 convert_element_type.358
  (164 shorter events, 84.1 us)
Async XLA Ops:
  6.5 5.0 %copy-start = (s32[64,16]{0,1:T(8,128)S(1)}, s32[64,16]{0,1:T(8,128)}, u32[]{:S(2)}) copy-start(s32[64,16]{0,1:T(8,128)} %param.10) | copy-start | bytes 12292
  6.5 125.6 %all-gather.2.cloned.1.call-start = ((), (), s32[]{:S(2)}) async-start(), calls=%async_computation.1 | async-start | bytes 21565440 | tf_op jit(solution)/shard_map/all_gather | solution.py:99
  7.3 300.4 %reduce-scatter.2.cloned.1.call-start = ((), (), s32[]{:S(2)}) async-start(), calls=%async_computation.2 | async-start | bytes 3604480 | tf_op jit(solution)/shard_map/reduce_scatter | solution.py:127
  256.6 6.0 %slice-start = ((s8[8388608]{0:T(1024)(128)(4,1)}), s8[4194304]{0:T(1024)(128)(4,1)S(1)}, s32[]{:S(2)}) async-start(s8[8388608]{0:T(1024)(128)(4,1)} %bitcast.53), calls=%async_computation.3 | async-start | bytes 8388608
  256.6 6.0 %copy-start.1 = (f32[8192]{0:T(1024)S(1)}, f32[8192]{0:T(1024)}, u32[]{:S(2)}) copy-start(f32[8192]{0:T(1024)} %param.13) | copy-start | bytes 98308
  256.6 6.0 %copy-start.2 = (f32[8192]{0:T(1024)S(1)}, f32[8192]{0:T(1024)}, u32[]{:S(2)}) copy-start(f32[8192]{0:T(1024)} %param.14) | copy-start | bytes 98308
  260.1 2.5 slice-start.1
Sparse Core Ops, SparseCore 0:
  9.9 122.2 all-gather.1
  272.3 35.2 reduce-scatter.1
where the time goes:
time: 318 us; the launch traced here: 316 us
  waiting for transfers between devices  151 us (47%)
  other arithmetic  60.5 us (19%)
  matrix products  43.5 us (14%)
  local copies, waits for them, and re-layouts  37 us (12%)
  between operations  13.6 us (4%)
  loops' own time  10.4 us (3%)
    all_gather x1, waiting for transfers between devices, per_device(): lax.all_gather(occluder_exit_radiance, 'cluster', axis=0, tiled=True)  115 us
    reduce_scatter x1, waiting for transfers between devices, per_device(): lax.psum_scatter(partial_sum, 'dir', scatter_dimension=1, tiled=True)  35.5 us
    select_n x16, other arithmetic, one_block(): weight = jnp.where(ray_codes < live_count, lit, 0.0)  28.3 us
    dot_general x16, matrix products, one_block(): return jnp.dot(stacked, spread, preferred_element_type=jnp.float32)  24.1 us
    convert_element_type x16, other arithmetic, one_block(): spread = jnp.where(onehot, weight[None, :, :], 0.0).astype(jnp.bfloat16)....  22.4 us
    dynamic_slice x16, local copies, waits for them, and re-layouts, one_block(): ray_codes = lax.dynamic_slice_in_dim(ray_code, first_vertex, block_width, 1)  17.3 us
    another operation x1, loops' own time, per_device(): pieces = lax.map(one_block, lax.iota(jnp.int32, block_count))  10.4 us
    dynamic_slice x16, local copies, waits for them, and re-layouts, per_device(): pieces = lax.map(one_block, lax.iota(jnp.int32, block_count))  10.3 us
  transfers between devices with their start and end apart: 2, of which 2 were waited for; matrix products, arithmetic and copies ran while one was open for 3% of the time, Pallas kernels for 0%

commit v1 on v0

--- a/solution.py
+++ b/solution.py
@@ -7,6 +7,11 @@
 NDIR = 1024
 SHORD = 9
 golden_angle = math.pi * (3.0 - math.sqrt(5.0))
+
+
+def gather_from_all(x, axis, dim):
+    copies = jnp.concatenate([x] * lax.axis_size(axis), axis=dim)
+    return lax.all_to_all(copies, axis, dim, dim, tiled=True)
 
 
 def sphere_points(direction_index, direction_overall_count):
@@ -96,7 +101,7 @@
     )
     own_list = occluder_list[own_cluster]
     slot_index = lax.iota(jnp.int32, slot_total)
-    portion_slice = lax.all_gather(occluder_exit_radiance, "cluster", axis=0, tiled=True)
+    portion_slice = gather_from_all(occluder_exit_radiance, "cluster", 0)
     selected_entries = own_list[:, None] == lax.iota(jnp.int32, portion_slice.shape[0])[None, :]
     entries = jnp.einsum(
         "fx,xwn->fwn",

time: 318 us -> 800 us (2.52)
  waiting for transfers between devices: 151 us -> 530 us
  local copies, waits for them, and re-layouts: 37 us -> 119 us
  starting transfers between devices: 0.04 us -> 13.5 us
    all_to_all x0 -> x1, waiting for transfers between devices: none -> 493 us  [gather_from_all(): return lax.all_to_all(copies, axis, dim, dim, tiled=True)]
    all_gather x1 -> x0, waiting for transfers between devices: 115 us -> none  [per_device(): lax.all_gather(occluder_exit_radiance, 'cluster', axis=0, tiled=True)]
    unnamed x14 -> x81, local copies, waits for them, and re-layouts: 2.81 us -> 85.9 us
    all_to_all x0 -> x1, starting transfers between devices: none -> 13.3 us  [gather_from_all(): return lax.all_to_all(copies, axis, dim, dim, tiled=True)]
  transfers between devices with their start and end apart: 2 -> 2, of which waited for: 2 -> 2; matrix products, arithmetic and copies ran while one was open for 3% -> 1% of each run, Pallas kernels for 0% -> 0%
where the time goes in v1:
time: 800 us; the launch traced here: 797 us
  waiting for transfers between devices  530 us (66%)
  local copies, waits for them, and re-layouts  119 us (15%)
  other arithmetic  60 us (8%)
  matrix products  49.9 us (6%)
  between operations  13.6 us (2%)
  starting transfers between devices  13.5 us (2%)
  loops' own time  10.6 us (1%)
    all_to_all x1, waiting for transfers between devices, gather_from_all(): return lax.all_to_all(copies, axis, dim, dim, tiled=True)  493 us
    unnamed x81, local copies, waits for them, and re-layouts  85.9 us
    reduce_scatter x1, waiting for transfers between devices, per_device(): lax.psum_scatter(partial_sum, 'dir', scatter_dimension=1, tiled=True)  37.2 us
    select_n x16, other arithmetic, one_block(): weight = jnp.where(ray_codes < live_count, lit, 0.0)  29.3 us
    dot_general x16, matrix products, one_block(): return jnp.dot(stacked, spread, preferred_element_type=jnp.float32)  24.1 us
    convert_element_type x16, other arithmetic, one_block(): spread = jnp.where(onehot, weight[None, :, :], 0.0).astype(jnp.bfloat16)....  22.4 us
    dynamic_slice x16, local copies, waits for them, and re-layouts, one_block(): ray_codes = lax.dynamic_slice_in_dim(ray_code, first_vertex, block_width, 1)  17.3 us
  transfers between devices with their start and end apart: 2, of which 2 were waited for; matrix products, arithmetic and copies ran while one was open for 1% of the time, Pallas kernels for 0%

profile of v1, /device:TPU:1, one launch (start us, length us, event | category | flops | bytes accessed | tf_op | source)
XLA Modules:
  0.0 797.1 jit_solution(16762627675640138851)
XLA Ops:
  6.5 1.9 constant_dynamic-update-slice_fusion.63
  90.5 13.3 %all-to-all-start = ((bf16[512,81,256]{2,1,0:T(8,128)(2,1)}), bf16[512,81,256]{2,1,0:T(8,128)(2,1)}, u32[]{:S(2)}, u32[]{:S(2)}) async-start(bf16[512,81,256]{2,1,0:T(8,128)(2,1)} %constant_dynamic-update-slice_fusion), calls=%async_computation | async-start | bytes 46137344 | tf_op jit(solution)/shard_map/all_to_all | solution.py:14
  108.0 3.5 add_maximum_fusion
  111.5 492.7 %all-to-all-done = bf16[512,81,256]{2,1,0:T(8,128)(2,1)} async-done(((bf16[512,81,256]{2,1,0:T(8,128)(2,1)}), bf16[512,81,256]{2,1,0:T(8,128)(2,1)}, u32[]{:S(2)}, u32[]{:S(2)}) %all-to-all-start) | async-done | bytes 21233696 | tf_op jit(solution)/shard_map/all_to_all | solution.py:14
  604.2 12.9 %fusion.12 = bf16[81,16,256]{2,1,0:T(8,128)(2,1)S(1)} fusion(bf16[512,81,256]{2,1,0:T(8,128)(2,1)} %all-to-all-done, s32[16]{0:T(128)S(1)} %dynamic-slice_reduce_fusion), kind=kOutput, calls=%fused_computation.18 | convolution fusion | flops 340078592 | bytes 21897280 | tf_op jit(solution)/shard_map/fx,xwn->fwn/dot_general | solution.py:106
  617.5 114.8 %while.12 = (s32[]{:T(128)}, f32[16,81,512]{2,1,0:T(8,128)}, s32[16]{0:T(128)S(1)}, s32[256,8192]{1,0:T(8,128)}, s32[]{:T(128)}, /*index=5*/bf16[256,8192]{1,0:T...) while((s32[]{:T(128)}, f32[16,81,512]{2,1,0:T(8,128)}, ...), condition=%wide.region_1.2_spmd.clone, body=%wide.region_0.1_spmd.clone.sunk | while | flops 344195072 | bytes 12182259 | solution.py:129
  618.7 1.8 dynamic-slice_select_fusion.2
  625.9 1.8 dynamic-slice_select_fusion.2
  633.1 1.8 dynamic-slice_select_fusion.2
  647.4 1.8 dynamic-slice_select_fusion.2
  654.6 1.8 dynamic-slice_select_fusion.2
  661.8 1.8 dynamic-slice_select_fusion.2
  668.9 1.8 dynamic-slice_select_fusion.2
  676.1 1.8 dynamic-slice_select_fusion.2
  683.3 1.8 dynamic-slice_select_fusion.2
  690.5 1.8 dynamic-slice_select_fusion.2
  697.6 1.8 dynamic-slice_select_fusion.2
  704.8 1.8 dynamic-slice_select_fusion.2
  712.0 1.8 dynamic-slice_select_fusion.2
  732.2 3.4 copy.75
  736.1 2.0 copy.78
  738.1 13.0 %fusion.4 = f32[81,8192]{1,0:T(8,128)} fusion(f32[81,256]{1,0:T(8,128)S(1)} %stack.5, s32[256,8192]{1,0:T(8,128)} %get-tuple-element.259, s32[]{:T(128)} %bitcast, f32[81,8192]{1,0:T(8,128)S(1)} %bitcast.53, f32[8192]{0:T(1024)S(1)} %copy-done.5, f32[8192]{0:T(1024)S(1)} %copy-done.3, f32[256]{0:T(256)S(1)} %multiply_subtract_fusion, ...), kind=kOutput, calls=%fused_computation.11 | convolution fusion | flops 2057199616 | bytes 13914116 | tf_op jit(solution)/shard_map/dot_general | solution.py:96
  751.1 37.2 %reduce-scatter.2.cloned.1.call-done = f32[81,2048]{1,0:T(8,128)} async-done(((f32[81,8192]{1,0:T(8,128)}), f32[81,2048]{1,0:T(8,128)}) %reduce-scatter.2.cloned.1.call-update) | async-done | bytes 663568 | tf_op jit(solution)/shard_map/reduce_scatter | solution.py:132
  788.3 1.9 convert_element_type.358
  (230 shorter events, 167.3 us)
Async XLA Ops:
  6.5 101.1 %copy-start = (s32[64,16]{0,1:T(8,128)S(1)}, s32[64,16]{0,1:T(8,128)}, u32[]{:S(2)}) copy-start(s32[64,16]{0,1:T(8,128)} %param.10) | copy-start | bytes 12292
  6.5 58.9 %copy-start.2 = (bf16[8,81,256]{2,0,1:T(8,128)(2,1)S(1)}, bf16[8,81,256]{2,0,1:T(8,128)(2,1)}, u32[]{:S(2)}) copy-start(bf16[8,81,256]{2,0,1:T(8,128)(2,1)} %param.15) | copy-start | bytes 995332
  90.5 13.5 %copy-start.6 = (s32[64]{0:T(128)S(1)}, s32[64]{0:T(128)}, u32[]{:S(2)}) copy-start(s32[64]{0:T(128)} %param.11) | copy-start | bytes 772
  90.5 17.4 %copy-start.3 = (f32[8192]{0:T(1024)S(1)}, f32[8192]{0:T(1024)}, u32[]{:S(2)}) copy-start(f32[8192]{0:T(1024)} %param.13) | copy-start | bytes 98308
  90.5 17.4 %copy-start.4 = (f32[8192]{0:T(1024)S(1)}, f32[8192]{0:T(1024)}, u32[]{:S(2)}) copy-start(f32[8192]{0:T(1024)} %param.12) | copy-start | bytes 98308
  90.5 513.8 %all-to-all-start = ((bf16[512,81,256]{2,1,0:T(8,128)(2,1)}), bf16[512,81,256]{2,1,0:T(8,128)(2,1)}, u32[]{:S(2)}, u32[]{:S(2)}) async-start(bf16[512,81,256]{2,1,0:T(8,128)(2,1)} %constant_dynamic-update-slice_fusion), calls=%async_computation | async-start | bytes 46137344 | tf_op jit(solution)/shard_map/all_to_all | solution.py:14
  103.8 684.6 %reduce-scatter.2.cloned.1.call-start = ((), (), s32[]{:S(2)}) async-start(), calls=%async_computation.2 | async-start | bytes 3604480 | tf_op jit(solution)/shard_map/reduce_scatter | solution.py:132
  617.4 120.6 %copy-start.5 = (f32[8192]{0:T(1024)S(1)}, f32[8192]{0:T(1024)}, u32[]{:S(2)}) copy-start(f32[8192]{0:T(1024)} %param.14) | copy-start | bytes 98308
  732.2 58.0 %copy-start.1 = (s32[64,16]{0,1:T(8,128)S(1)}, s32[64,16]{0,1:T(8,128)}, u32[]{:S(2)}) copy-start(s32[64,16]{0,1:T(8,128)} %param.10) | copy-start | bytes 12292
Sparse Core Ops, SparseCore 0:
  751.2 37.0 reduce-scatter.1
